TPU v7x, 32 devices: a whole 2x2x4 slice. The times are simulated.
32 devices in a mesh: seq: 16 (over z, y, x), img: 2 (over core).
Axes of the slice: x: 2, y: 2, z: 4, core: 2. Of those that a mesh axis runs over, the one named last changes fastest.
Arguments:
- inner_acts: bfloat16 [4096, 3072], P(('img', 'seq')), parts along dimension 0, may hold values from -6 to 6
- gate_acts: bfloat16 [4096, 3072], P(('img', 'seq')), parts along dimension 0, may hold values from -6 to 6
- state_proj: bfloat16 [4096, 64], P(('img', 'seq')), parts along dimension 0, may hold values from -3 to 3
- step_raw: bfloat16 [4096, 96], P(('img', 'seq')), parts along dimension 0, may hold values from -4 to 4
- conv_weight: float32 [2, 4, 3072], replicated, may hold values from -3 to 3
- conv_bias: float32 [2, 3072], replicated, may hold values from -3 to 3
- step_bias: float32 [2, 48], replicated, may hold values from -1.5 to 0.5
- decay_rate: float32 [2, 48], replicated, may hold values from 5e-06 to 0.04
- skip_gain: float32 [2, 48], replicated, may hold values from 0.5 to 2
- norm_gain: float32 [3072], replicated, may hold values from 0.5 to 1.5
Outputs:
- mixed: bfloat16 [4096, 3072], P(('img', 'seq')), parts along dimension 0
There are 2 independent parts, one for each index of `img`. A program takes and returns all parts, laid end to end along the dimension named above; an argument that names none is the same for every part. Nothing has to cross between parts.
All inputs are finite; a program needn't handle non-finite values.
Results may differ from a plain program's by a relative error of at most 0.0058.
Values may be sent and summed in bfloat16 or wider, within the bound.
No kernel may reach another device: no remote copies, remote signals or barrier semaphores. Data moves between devices by JAX's collectives and lax.ppermute only.
A program may use at most 192 MiB of HBM per device.

v0:
```python
import jax
import jax.numpy as jnp
from jax import lax
from jax.sharding import PartitionSpec as P


def extended(cells, sides, width):
    for axis, dim in sides:
        count = lax.axis_size(axis)
        ends = count - 1
        head = lax.slice_in_dim(cells, 0, width, axis=dim)
        tail = lax.slice_in_dim(cells, cells.shape[dim] - width, cells.shape[dim], axis=dim)
        cells = jnp.concatenate(
            [
                lax.ppermute(tail, axis, [(i, (i + 1) % count) for i in range(ends)]),
                cells,
                lax.ppermute(head, axis, [((i + 1) % count, i) for i in range(ends)]),
            ],
            axis=dim,
        )
    return cells


def prefix(value, axis, join, neutral, backward):
    count, mine = (lax.axis_size(axis), lax.axis_index(axis))
    pieces = jax.tree.map(lambda part: lax.all_gather(part, axis), value)
    if backward:
        pieces = jax.tree.map(lambda part: part[::-1], pieces)
        mine = count - 1 - mine
    running = jax.tree.map(
        lambda part, zero: jnp.full_like(part, 0) + jnp.asarray(zero, part.dtype), value, neutral
    )

    def lap(position, running):
        longer = join(running, jax.tree.map(lambda part: part[position], pieces))
        return jax.tree.map(lambda new, old: jnp.where(position < mine, new, old), longer, running)

    return lax.fori_loop(0, count - 1, lap, running)


def convolve(window, weight, bias):
    kernel = weight.shape[0]
    length = window.shape[0] - kernel + 1
    accum = jnp.zeros((length, window.shape[1]), jnp.float32) + bias[None, :]
    for offset in range(kernel):
        start = kernel - 1 - offset
        accum = accum + weight[offset][None, :] * window[start : start + length].astype(jnp.float32)
    return jax.nn.silu(accum).astype(jnp.bfloat16)


def local_terms(window, write_rows, read_rows, raw_step, weight, bias, step_bias, rate, skip):
    conved = convolve(window, weight, bias)
    length, width = conved.shape
    heads = raw_step.shape[1]
    step_size = jax.nn.softplus(raw_step.astype(jnp.float32) + step_bias[None, :])
    cumul = jnp.cumsum(-rate[None, :] * step_size, axis=0)
    later = lax.broadcasted_iota(jnp.int32, (length, length), 0)
    earlier = lax.broadcasted_iota(jnp.int32, (length, length), 1)
    causal = (later >= earlier)[None]
    spread = cumul.T[:, :, None] - cumul.T[:, None, :]
    decay = jnp.where(causal, jnp.exp(jnp.where(causal, spread, 0.0)), 0.0)
    scores = jnp.dot(read_rows, write_rows.T, preferred_element_type=jnp.float32)
    weights = (scores[None] * decay * step_size.T[:, None, :]).astype(jnp.bfloat16)
    per_head = conved.reshape(length, heads, width // heads)
    inside = jnp.einsum("hts,shp->thp", weights, per_head, preferred_element_type=jnp.float32)
    final_log = cumul[-1]
    carried = jnp.exp(final_log[None, :] - cumul) * step_size
    loaded = (carried[:, :, None] * write_rows.astype(jnp.float32)[:, None, :]).astype(jnp.bfloat16)
    end_state = jnp.einsum("shp,shn->hpn", per_head, loaded, preferred_element_type=jnp.float32)
    base = inside + skip[None, :, None] * per_head.astype(jnp.float32)
    return (base, cumul, jnp.exp(final_log), end_state)


def inter_terms(cumul, read_rows, incoming):
    readout = jnp.einsum(
        "tn,hpn->thp", read_rows.astype(jnp.float32), incoming, precision=lax.Precision.HIGHEST
    )
    return readout * jnp.exp(cumul)[:, :, None]


def combine_carry(earlier, later):
    return (earlier[0] * later[0], later[0][:, None, None] * earlier[1] + later[1])


def local(
    inner_acts,
    gate_acts,
    state_proj,
    step_raw,
    conv_weight,
    conv_bias,
    step_bias,
    decay_rate,
    skip_gain,
    norm_gain,
):
    kernel = conv_weight.shape[1]
    length, width = inner_acts.shape
    state_dim = state_proj.shape[1] // 4
    heads = step_raw.shape[1] // 2
    padded = extended(inner_acts, (("seq", 0),), kernel - 1)
    ahead = padded[: length + kernel - 1]
    behind = padded[::-1][: length + kernel - 1]
    flipped_proj = state_proj[::-1]
    flipped_raw = step_raw[::-1]
    forward_base, forward_log, forward_total, forward_end = local_terms(
        ahead,
        state_proj[:, 0:state_dim],
        state_proj[:, state_dim : 2 * state_dim],
        step_raw[:, :heads],
        conv_weight[0],
        conv_bias[0],
        step_bias[0],
        decay_rate[0],
        skip_gain[0],
    )
    backward_base, backward_log, backward_total, backward_end = local_terms(
        behind,
        flipped_proj[:, 2 * state_dim : 3 * state_dim],
        flipped_proj[:, 3 * state_dim : 4 * state_dim],
        flipped_raw[:, heads:],
        conv_weight[1],
        conv_bias[1],
        step_bias[1],
        decay_rate[1],
        skip_gain[1],
    )
    forward_enter = prefix(
        (forward_total, forward_end),
        "seq",
        combine_carry,
        (jnp.ones_like(forward_total), jnp.zeros_like(forward_end)),
        False,
    )[1]
    backward_enter = prefix(
        (backward_total, backward_end),
        "seq",
        combine_carry,
        (jnp.ones_like(backward_total), jnp.zeros_like(backward_end)),
        True,
    )[1]
    forward = (
        forward_base
        + inter_terms(forward_log, state_proj[:, state_dim : 2 * state_dim], forward_enter)
    ).reshape(length, width)
    backward = (
        backward_base
        + inter_terms(backward_log, flipped_proj[:, 3 * state_dim : 4 * state_dim], backward_enter)
    ).reshape(length, width)[::-1]
    gated = (forward + backward) * jax.nn.silu(gate_acts.astype(jnp.float32))
    scale = lax.rsqrt(jnp.mean(gated * gated, axis=1, keepdims=True) + 1e-05)
    return (gated * scale * norm_gain[None, :]).astype(jnp.bfloat16)


def solution(mesh):
    return jax.shard_map(
        local,
        mesh=mesh,
        in_specs=(
            P(("img", "seq"), None),
            P(("img", "seq"), None),
            P(("img", "seq"), None),
            P(("img", "seq"), None),
            P(),
            P(),
            P(),
            P(),
            P(),
            P(),
        ),
        out_specs=P(("img", "seq"), None),
        check_vma=False,
    )
```

profile of v0, /device:TPU:0, one launch (start us, length us, event | category | flops | bytes accessed | tf_op | source)
XLA Modules:
  0.0 292.6 jit_solution(16704680512442306595)
XLA Ops:
  6.6 1.6 fusion.42
  8.2 1.3 collective-permute-start.1
  9.5 1.2 constant_dynamic-update-slice_fusion.1
  15.1 7.8 %slice.163 = bf16[128,3072]{1,0:T(8,128)(2,1)} reverse(bf16[128,3072]{1,0:T(8,128)(2,1)S(1)} %copy-done), dimensions={0} | reverse | bytes 1572864 | tf_op jit(solution)/shard_map/slice | solution.py:47
  24.3 1.4 fusion.41
  25.6 12.0 %slice.167 = bf16[128,3072]{1,0:T(8,128)(2,1)} reverse(bf16[128,3072]{1,0:T(8,128)(2,1)} %get-tuple-element.253), dimensions={0} | reverse | bytes 1572864 | tf_op jit(solution)/shard_map/slice | solution.py:47
  37.6 7.8 %slice.170 = bf16[128,3072]{1,0:T(8,128)(2,1)} reverse(bf16[128,3072]{1,0:T(8,128)(2,1)S(1)} %get-tuple-element.255), dimensions={0} | reverse | bytes 1572864 | tf_op jit(solution)/shard_map/slice | solution.py:47
  45.4 7.7 %slice.173 = bf16[128,3072]{1,0:T(8,128)(2,1)} reverse(bf16[128,3072]{1,0:T(8,128)(2,1)S(1)} %get-tuple-element.254), dimensions={0} | reverse | bytes 1572864 | tf_op jit(solution)/shard_map/slice | solution.py:47
  53.1 2.3 multiply_convert_fusion.5
  56.1 1.3 fusion.25
  57.5 5.5 %collective-permute-start = (bf16[3,3072]{1,0:T(4,128)(2,1)S(1)}, bf16[3,3072]{1,0:T(4,128)(2,1)S(1)}, u32[]{:S(2)}, u32[]{:S(2)}) collective-permute-start(bf16[3,3072]{1,0:T(4,128)(2,1)S(1)} %copy-done.24), channel_id=1, source_target_pairs={{0,2},{2,4},{4,6},{6,8},{8,10},{10,12},{12,14},{14,16},{16,18},{18... | collective-permute-start | bytes 55304 | tf_op jit(solution)/shard_map/ppermute | solution.py:15
  65.1 39.6 %all-gather.3 = f32[16,1,48]{2,1,0:T(1,128)S(1)} all-gather(f32[1,1,48]{2,1,0:T(1,128)S(1)} %copy-done.34), channel_id=1, replica_groups=mesh['seq'=16,'img'=2] {'seq'}, dimensions={0}, use_global_device_ids=true | all-gather | bytes 3264 | tf_op jit(solution)/shard_map/all_gather | solution.py:26
  106.3 38.5 %all-gather.2 = f32[16,1,48]{2,1,0:T(1,128)} all-gather(f32[1,1,48]{2,1,0:T(1,128)S(1)} %get-tuple-element.273), channel_id=1, replica_groups=mesh['seq'=16,'img'=2] {'seq'}, dimensions={0}, use_global_device_ids=true | all-gather | bytes 3264 | tf_op jit(solution)/shard_map/all_gather | solution.py:26
  146.3 1.3 fusion.24
  147.6 2.7 fusion.3
  150.4 2.7 fusion.2
  153.1 2.0 all-gather.9.cloned.1.call-done
  155.0 5.9 %rev.13 = f32[16,48,64,16]{2,3,1,0:T(8,128)} reverse(f32[16,48,64,16]{2,3,1,0:T(8,128)} %bitcast.100), dimensions={0} | reverse | bytes 6291456 | tf_op jit(solution)/shard_map/rev | solution.py:28
  161.0 27.9 %while.29 = (s32[]{:T(128)}, f32[48,64,16]{1,2,0:T(8,128)S(1)}, s32[]{:T(128)}, f32[16,48]{1,0:T(8,128)}, f32[16,48,64,16]{2,3,1,0:T(8,128)}, /*index=5*/s32[]{:T(128)}, s32[]{:T(128)}) while((s32[]{:T(128)}, f32[48,64,16]{1,2,0:T(8,128)S(1)}, s32[]{:T(128)}, f32[16,48]{1,0:T(8,128)}, f32[16,48,64,16]{2,3,1,0:T(8,128)}, ...), condition=%wide.region_5.6_spmd.clone, body=%wide.region_4.5_spmd.clone.sunk | while | flops 196612 | bytes 590505 | solution.py:38
  163.5 1.2 fusion.61
  165.4 1.2 fusion.61
  171.0 1.2 fusion.61
  180.3 1.2 fusion.61
  184.0 1.2 fusion.61
  188.9 4.2 %fusion.8 = f32[128,48,64]{0,2,1:T(8,128)} fusion(f32[48,64,128]{2,1,0:T(8,128)} %fusion.3, bf16[128,48,64]{0,2,1:T(8,128)(2,1)S(1)} %bitcast.96, f32[48,64,16]{1,2,0:T(8,128)S(1)} %get-tuple-element.194, f32[128,48]{0,1:T(8,128)S(1)} %copy.40, f32[48]{0:T(128)S(1)} %get-tuple-element.283, bf16[128,16]{0,1:T(8,128)(2,1)S(1)} %slice.175), kind=kOutput, calls=%fused_computation.17 | convolution fusion | flops 77463552 | bytes 4157632 | tf_op jit(solution)/shard_map/tn,hpn->thp/dot_general | solution.py:75
  193.1 1.9 copy.41
  195.0 7.8 %rev.14 = f32[128,3072]{1,0:T(8,128)} reverse(f32[128,3072]{1,0:T(8,128)S(1)} %copy.41), dimensions={0} | reverse | bytes 3145728 | tf_op jit(solution)/shard_map/rev | solution.py:146
  202.9 47.0 %all-gather.7.cloned.1.call-done = f32[768,64,16]{1,2,0:T(8,128)} async-done(((f32[48,64,16]{1,2,0:T(8,128)}), f32[768,64,16]{1,2,0:T(8,128)}) %all-gather.7.cloned.1.call-update) | async-done | bytes 3145744 | tf_op jit(solution)/shard_map/all_gather | solution.py:26
  249.8 27.8 %while.28 = (s32[]{:T(128)}, f32[48,64,16]{1,2,0:T(8,128)S(1)}, s32[]{:T(128)}, f32[16,48]{1,0:T(8,128)}, f32[16,48,64,16]{2,3,1,0:T(8,128)}, /*index=5*/s32[]{:T(128)}, s32[]{:T(128)}) while((s32[]{:T(128)}, f32[48,64,16]{1,2,0:T(8,128)S(1)}, s32[]{:T(128)}, f32[16,48]{1,0:T(8,128)}, f32[16,48,64,16]{2,3,1,0:T(8,128)}, ...), condition=%wide.region_2.3_spmd.clone, body=%wide.region_1.2_spmd.clone.sunk | while | flops 196612 | bytes 590505 | solution.py:38
  277.7 3.0 %fusion.9 = f32[128,48,64]{0,2,1:T(8,128)S(1)} fusion(f32[48,64,128]{2,1,0:T(8,128)} %fusion.2, bf16[128,48,64]{0,2,1:T(8,128)(2,1)S(1)} %bitcast.99, f32[48,64,16]{1,2,0:T(8,128)S(1)} %get-tuple-element.193, f32[128,48]{0,1:T(8,128)S(1)} %copy-done.11, f32[48]{0:T(128)S(1)} %copy-done.30, bf16[128,64]{0,1:T(8,128)(2,1)} %param.16), kind=kOutput, calls=%fused_computation.20 | convolution fusion | flops 77463552 | bytes 4157632 | tf_op jit(solution)/shard_map/tn,hpn->thp/dot_general | solution.py:75
  280.7 1.6 copy.42
  282.3 2.3 multiply_reduce_fusion
  (171 shorter events, 62.0 us)
Async XLA Ops:
  6.5 8.6 %copy-start = (bf16[128,3072]{1,0:T(8,128)(2,1)S(1)}, bf16[128,3072]{1,0:T(8,128)(2,1)}, u32[]{:S(2)}) copy-start(bf16[128,3072]{1,0:T(8,128)(2,1)} %param.14) | copy-start | bytes 2359300
  6.5 4.1 %copy-start.12 = (f32[2,4,3072]{2,1,0:T(4,128)S(1)}, f32[2,4,3072]{2,1,0:T(4,128)}, u32[]{:S(2)}) copy-start(f32[2,4,3072]{2,1,0:T(4,128)} %param.18) | copy-start | bytes 294916
  6.5 4.8 %copy-start.22 = (f32[2,3072]{1,0:T(2,128)S(1)}, f32[2,3072]{1,0:T(2,128)}, u32[]{:S(2)}) copy-start(f32[2,3072]{1,0:T(2,128)} %param.19) | copy-start | bytes 73732
  6.5 5.4 %copy-start.23 = (bf16[128,96]{0,1:T(8,128)(2,1)S(1)}, bf16[128,96]{0,1:T(8,128)(2,1)}, u32[]{:S(2)}) copy-start(bf16[128,96]{0,1:T(8,128)(2,1)} %param.17) | copy-start | bytes 73732
  6.5 5.7 %copy-start.31 = (f32[2,48]{1,0:T(2,128)S(1)}, f32[2,48]{1,0:T(2,128)}, u32[]{:S(2)}) copy-start(f32[2,48]{1,0:T(2,128)} %param.20) | copy-start | bytes 1156
  6.5 5.7 %copy-start.32 = (f32[2,48]{1,0:T(2,128)S(1)}, f32[2,48]{1,0:T(2,128)}, u32[]{:S(2)}) copy-start(f32[2,48]{1,0:T(2,128)} %param.21) | copy-start | bytes 1156
  6.6 8.0 %copy-start.18 = (bf16[128,64]{0,1:T(8,128)(2,1)S(1)}, bf16[128,64]{0,1:T(8,128)(2,1)}, u32[]{:S(2)}) copy-start(bf16[128,64]{0,1:T(8,128)(2,1)} %param.16) | copy-start | bytes 49156
  6.6 148.5 %all-gather.9.cloned.1.call-start = ((), (), s32[]{:S(2)}) async-start(), calls=%async_computation.1 | async-start | bytes 6684672 | tf_op jit(solution)/shard_map/all_gather | solution.py:26
  8.2 16.0 %collective-permute-start.1 = (bf16[3,3072]{1,0:T(4,128)(2,1)S(1)}, bf16[3,3072]{1,0:T(4,128)(2,1)S(1)}, u32[]{:S(2)}, u32[]{:S(2)}) collective-permute-start(bf16[3,3072]{1,0:T(4,128)(2,1)S(1)} %get-tuple-element.256), channel_id=1, source_target_pairs={{2,0},{4,2},{6,4},{8,6},{10,8},{12,10},{14,12},{16,14},{18,16},{20... | collective-permute-start | bytes 55304 | tf_op jit(solution)/shard_map/ppermute | solution.py:17
  13.2 12.4 %copy-start.4 = (f32[128,48]{1,0:T(8,128)}, f32[128,48]{1,0:T(8,128)S(1)}, u32[]{:S(2)}) copy-start(f32[128,48]{1,0:T(8,128)S(1)} %reduce_window_sum.18) | copy-start | bytes 73732
  37.6 15.5 %copy-start.2 = (bf16[128,3072]{1,0:T(8,128)(2,1)S(1)}, bf16[128,3072]{1,0:T(8,128)(2,1)}, u32[]{:S(2)}) copy-start(bf16[128,3072]{1,0:T(8,128)(2,1)} %slice.163) | copy-start | bytes 2359300
  45.4 7.7 %copy-start.3 = (bf16[128,3072]{1,0:T(8,128)(2,1)S(1)}, bf16[128,3072]{1,0:T(8,128)(2,1)}, u32[]{:S(2)}) copy-start(bf16[128,3072]{1,0:T(8,128)(2,1)} %slice.167) | copy-start | bytes 2359300
  55.4 2.1 copy-start.24
  55.4 7.6 %copy-start.25 = (bf16[128,16]{0,1:T(8,128)(2,1)S(1)}, bf16[128,16]{0,1:T(8,128)(2,1)}, u32[]{:S(2)}) copy-start(bf16[128,16]{0,1:T(8,128)(2,1)} %get-tuple-element.282) | copy-start | bytes 12292
  55.4 7.7 %copy-start.8 = (f32[128,48]{1,0:T(8,128)S(1)}, f32[128,48]{1,0:T(8,128)}, u32[]{:S(2)}) copy-start(f32[128,48]{1,0:T(8,128)} %get-tuple-element.290) | copy-start | bytes 73732
  55.4 7.9 %copy-start.33 = (f32[2,48]{1,0:T(2,128)S(1)}, f32[2,48]{1,0:T(2,128)}, u32[]{:S(2)}) copy-start(f32[2,48]{1,0:T(2,128)} %param.22) | copy-start | bytes 1156
  55.4 8.4 %copy-start.19 = (bf16[128,64]{0,1:T(8,128)(2,1)S(1)}, bf16[128,64]{0,1:T(8,128)(2,1)}, u32[]{:S(2)}) copy-start(bf16[128,64]{0,1:T(8,128)(2,1)} %param.16) | copy-start | bytes 49156
  55.4 8.7 %copy-start.7 = (bf16[128,48]{1,0:T(8,128)(2,1)S(1)}, bf16[128,48]{1,0:T(8,128)(2,1)}, u32[]{:S(2)}) copy-start(bf16[128,48]{1,0:T(8,128)(2,1)} %copy-done.6) | copy-start | bytes 36868
  55.4 8.7 %copy-start.29 = (f32[48]{0:T(128)S(1)}, f32[48]{0:T(128)}, u32[]{:S(2)}) copy-start(f32[48]{0:T(128)} %copy-done.28) | copy-start | bytes 580
  55.5 9.4 %copy-start.10 = (f32[48,128]{0,1:T(8,128)S(1)}, f32[48,128]{0,1:T(8,128)}, u32[]{:S(2)}) copy-start(f32[48,128]{0,1:T(8,128)} %get-tuple-element.275) | copy-start | bytes 73732
  55.5 9.5 %copy-start.5 = (f32[128,48]{1,0:T(8,128)S(1)}, f32[128,48]{1,0:T(8,128)}, u32[]{:S(2)}) copy-start(f32[128,48]{1,0:T(8,128)} %copy-done.4) | copy-start | bytes 73732
  55.9 9.2 %copy-start.34 = (f32[1,1,48]{2,1,0:T(1,128)S(1)}, f32[1,1,48]{2,1,0:T(1,128)}, u32[]{:S(2)}) copy-start(f32[1,1,48]{2,1,0:T(1,128)} %get-tuple-element.269) | copy-start | bytes 580
  55.9 49.4 %copy-start.9 = (f32[128,48]{1,0:T(8,128)S(1)}, f32[128,48]{1,0:T(8,128)}, u32[]{:S(2)}) copy-start(f32[128,48]{1,0:T(8,128)} %get-tuple-element.266) | copy-start | bytes 73732
  55.9 88.9 %copy-start.14 = (f32[1,1,3072]{2,1,0:T(1,128)S(1)}, f32[1,1,3072]{2,1,0:T(1,128)}, u32[]{:S(2)}) copy-start(f32[1,1,3072]{2,1,0:T(1,128)} %get-tuple-element.261) | copy-start | bytes 36868
  55.9 88.9 %copy-start.15 = (f32[1,1,3072]{2,1,0:T(1,128)S(1)}, f32[1,1,3072]{2,1,0:T(1,128)}, u32[]{:S(2)}) copy-start(f32[1,1,3072]{2,1,0:T(1,128)} %get-tuple-element.262) | copy-start | bytes 36868
  55.9 88.9 %copy-start.16 = (f32[1,1,3072]{2,1,0:T(1,128)S(1)}, f32[1,1,3072]{2,1,0:T(1,128)}, u32[]{:S(2)}) copy-start(f32[1,1,3072]{2,1,0:T(1,128)} %get-tuple-element.263) | copy-start | bytes 36868
  55.9 88.9 %copy-start.17 = (f32[1,3072]{1,0:T(1,128)S(1)}, f32[1,3072]{1,0:T(1,128)}, u32[]{:S(2)}) copy-start(f32[1,3072]{1,0:T(1,128)} %get-tuple-element.279) | copy-start | bytes 36868
  57.4 192.4 %all-gather.7.cloned.1.call-start = ((), (), s32[]{:S(2)}) async-start(), calls=%async_computation | async-start | bytes 6684672 | tf_op jit(solution)/shard_map/all_gather | solution.py:26
  57.5 87.3 %collective-permute-start = (bf16[3,3072]{1,0:T(4,128)(2,1)S(1)}, bf16[3,3072]{1,0:T(4,128)(2,1)S(1)}, u32[]{:S(2)}, u32[]{:S(2)}) collective-permute-start(bf16[3,3072]{1,0:T(4,128)(2,1)S(1)} %copy-done.24), channel_id=1, source_target_pairs={{0,2},{2,4},{4,6},{6,8},{8,10},{10,12},{12,14},{14,16},{16,18},{18... | collective-permute-start | bytes 55304 | tf_op jit(solution)/shard_map/ppermute | solution.py:15
  249.8 27.8 %copy-start.11 = (f32[128,48]{0,1:T(8,128)S(1)}, f32[128,48]{0,1:T(8,128)}, u32[]{:S(2)}) copy-start(f32[128,48]{0,1:T(8,128)} %copy.33) | copy-start | bytes 73732
  249.8 27.8 %copy-start.30 = (f32[48]{0:T(128)S(1)}, f32[48]{0:T(128)}, u32[]{:S(2)}) copy-start(f32[48]{0:T(128)} %get-tuple-element.284) | copy-start | bytes 580
  282.3 2.3 copy-start.27
  (7 other events, 7.8 us)
Sparse Core Ops, SparseCore 0:
  57.5 97.4 all-gather.8
  157.8 91.9 all-gather.6
where the time goes:
time: 296 us; the launch traced here: 293 us
  local copies, waits for them, and re-layouts  83.6 us (28%)
  blocking collectives  78.1 us (26%)
  waiting for transfers between devices  49 us (17%)
  other arithmetic  45 us (15%)
  matrix products  15.6 us (5%)
  between operations  13.9 us (5%)
  starting transfers between devices  6.86 us (2%)
    all_gather x2, blocking collectives, prefix(): pieces = jax.tree.map(lambda part: lax.all_gather(part, axis), value)  78.1 us
    all_gather x2, waiting for transfers between devices, prefix(): pieces = jax.tree.map(lambda part: lax.all_gather(part, axis), value)  48.9 us
    slice x5, local copies, waits for them, and re-layouts, convolve(): window[start:start + length].astype(jnp.float32)  36.6 us
    select_n x30, other arithmetic, lap(): jnp.where(position < mine, new, old)  34.6 us
    mul x30, local copies, waits for them, and re-layouts, combine_carry(): later[0][:, None, None] * earlier[1] + later[1]  20.5 us
    rev x1, local copies, waits for them, and re-layouts, local(): (backward_base + inter_terms(backward_log, flipped_proj[:, 3 * state_dim:...  7.85 us
    dot_general x2, matrix products, inter_terms(): jnp.einsum('tn,hpn->thp', read_rows.astype(jnp.float32), incoming, precis...  7.22 us
    rev x2, local copies, waits for them, and re-layouts, prefix(): pieces = jax.tree.map(lambda part: part[::-1], pieces)  6.54 us
  transfers between devices with their start and end apart: 4, of which 2 were waited for; matrix products, arithmetic and copies ran while one was open for 25% of the time, Pallas kernels for 0%

commit v1 on v0

v1 whole, which is shorter than its diff:
```python
import functools
import jax
import jax.numpy as jnp
from jax import lax
from jax.experimental import pallas as pl
from jax.experimental.pallas import tpu as pltpu
from jax.sharding import PartitionSpec as P

F32, BF16 = jnp.float32, jnp.bfloat16
LANES = 128
SUB = 8


def partner(me, k, count):
    if count & (count - 1) == 0:
        return me ^ k, me ^ k
    return lax.rem(me - k + count, count), lax.rem(me + k, count)


def pairs(k, count, stride, total):
    out = []
    for i in range(total):
        pos = (i // stride) % count
        dest = pos ^ k if count & (count - 1) == 0 else (pos + k) % count
        out.append((i, i + (dest - pos) * stride))
    return out


def silu(v):
    h = 0.5 * v
    return h + h * jnp.tanh(h)


def softplus(v):
    return jnp.maximum(v, 0.0) + jnp.log1p(jnp.exp(-jnp.abs(v)))


def split(v, parts):
    out = []
    for _ in range(parts):
        top = v.astype(BF16)
        out.append(top)
        v = v - top.astype(F32)
    return out


def dot(a, b, dims=(((1,), (0,)), ((), ()))):
    return lax.dot_general(a, b, dims, preferred_element_type=F32)


def rows_of(shape):
    return lax.broadcasted_iota(jnp.int32, shape, 0)


def lanes_of(shape):
    return lax.broadcasted_iota(jnp.int32, shape, 1)


def spread(rows, repeat, head, start, width):
    r, c = rows_of((rows, width)), lanes_of((rows, width)) + start
    if repeat < rows:
        r = jnp.where(r >= repeat, r - repeat, r)
    first = r * head
    return jnp.where((c >= first) & (c < first + head), 1.0, 0.0).astype(BF16)


def doubled(v):
    return jnp.concatenate(split(v, 2), axis=1)


def scan_parts(d, raw_ref, bias_ref, rate_ref):
    heads = raw_ref.shape[1] // 2
    length = raw_ref.shape[0]
    raw = raw_ref[:, d * heads : (d + 1) * heads].astype(F32)
    step = softplus(raw + bias_ref[d : d + 1, :])
    t, s = rows_of((length, length)), lanes_of((length, length))
    tri = jnp.where(s <= t if d == 0 else s >= t, 1.0, 0.0)
    cumul = jnp.dot(
        tri, -rate_ref[d : d + 1, :] * step, precision=lax.Precision.HIGHEST,
        preferred_element_type=F32,
    )
    return step, cumul


def projections(d, proj_ref):
    state = proj_ref.shape[1] // 4
    write = proj_ref[:, 2 * d * state : (2 * d + 1) * state]
    read = proj_ref[:, (2 * d + 1) * state : (2 * d + 2) * state]
    return write, read


def conv_rows(d, x, cw_ref, cb_ref, lanes):
    length = x.shape[0]
    taps = cw_ref.shape[1]
    acc = cb_ref[d : d + 1, lanes] + cw_ref[d, 0:1, lanes] * x
    for k in range(1, taps):
        moved = pltpu.roll(x, k if d == 0 else length - k, 0)
        acc = acc + cw_ref[d, k : k + 1, lanes] * moved
    return silu(acc).astype(BF16)


def edge_conv(d, window, cw_ref, cb_ref, lanes):
    taps = cw_ref.shape[1]
    acc = cb_ref[d : d + 1, lanes]
    for k in range(taps):
        shift = taps - 1 - k if d == 0 else k
        moved = window if shift == 0 else pltpu.roll(window, SUB - shift, 0)
        acc = acc + cw_ref[d, k : k + 1, lanes] * moved
    return silu(acc).astype(BF16)


def edge_mask(d, length, taps):
    t = rows_of((length, 1))
    return t >= taps - 1 if d == 0 else t < length - (taps - 1)


def coef_rows(blocks, per_row):
    return -(-blocks // per_row)


def place(tile, coefs, per_row, block, first_row):
    row = rows_of(tile.shape)
    for j in range(SUB - first_row):
        index = j * per_row + block
        if index < len(coefs):
            tile = jnp.where(row == first_row + j, coefs[index], tile)
    return tile


def fetch(tile, index, per_row, first_row):
    j, block = divmod(index, per_row)
    return tile[first_row + j : first_row + j + 1, block * LANES : (block + 1) * LANES]


def stacked(rows):
    row = rows_of((SUB, rows[0].shape[1]))
    out = jnp.zeros((SUB, rows[0].shape[1]), F32)
    for j, value in enumerate(rows):
        out = jnp.where(row == j, value, out)
    return out


def widen(v):
    pad = LANES - v.shape[1]
    return jnp.concatenate([v, jnp.zeros((v.shape[0], pad), F32)], axis=1)


def ends_kernel(dims, x_ref, proj_ref, raw_ref, cw_ref, cb_ref, bias_ref, rate_ref, *outs):
    group, head, chunk, axis = dims
    length, width = x_ref.shape
    heads = raw_ref.shape[1] // 2
    taps = cw_ref.shape[1]
    state = proj_ref.shape[1] // 4
    edge = taps - 1
    part = width // group
    per_row = part // LANES
    me = lax.rem(lax.axis_index(axis), group)
    carried, writes, coefs, logs = [], [], [], []
    for d in range(2):
        step, cumul = scan_parts(d, raw_ref, bias_ref, rate_ref)
        last = cumul[length - 1 : length] if d == 0 else cumul[0:1]
        weight = jnp.exp(last - cumul) * step
        carried.append(doubled(jnp.where(edge_mask(d, length, taps), weight, 0.0)))
        write = projections(d, proj_ref)[0]
        writes.append(write)
        for j in range(edge):
            r = j if d == 0 else length - edge + j
            coefs.append(
                widen(
                    jnp.concatenate([weight[r : r + 1], write.astype(F32)[r : r + 1]], axis=1)
                )
            )
        logs += [widen(p.astype(F32)) for p in split(last, 3)]
    coefs = coefs + logs
    for k in range(group):
        out_ref = outs[k]
        target = partner(me, k, group)[1]
        for j in range(part // chunk):
            start = pl.multiple_of(target * part + j * chunk, chunk)
            lanes = pl.ds(start, chunk)
            here = slice(j * chunk, (j + 1) * chunk)
            x = x_ref[:, lanes].astype(F32)
            match = spread(2 * heads, heads, head, start, chunk)
            for d in range(2):
                conved = conv_rows(d, x, cw_ref, cb_ref, lanes)
                loaded = (conved.astype(F32) * dot(carried[d], match)).astype(BF16)
                end = dot(writes[d], loaded, (((0,), (0,)), ((), ())))
                out_ref[d * state : (d + 1) * state, here] = end.astype(BF16)
            row = rows_of((SUB, chunk))
            tail = pltpu.roll(x[length - SUB :], SUB - (SUB - 2 * edge), 0)
            tile = jnp.where(row < edge, x[:SUB], jnp.where(row < 2 * edge, tail, 0.0))
            for i in range(chunk // LANES):
                block = j * (chunk // LANES) + i
                piece = place(
                    tile[:, i * LANES : (i + 1) * LANES], coefs, per_row, block, 2 * edge
                )
                out_ref[2 * state :, block * LANES : (block + 1) * LANES] = piece.astype(BF16)


def inside_kernel(
    dims, x_ref, proj_ref, raw_ref, cw_ref, cb_ref, bias_ref, rate_ref, skip_ref, y_ref
):
    group, head, chunk, axis = dims
    length, width = x_ref.shape
    heads = raw_ref.shape[1] // 2
    taps = cw_ref.shape[1]
    t, s = rows_of((length, length)), lanes_of((length, length))
    before, after, mixes, skips, masks = [], [], [], [], []
    for d in range(2):
        step, cumul = scan_parts(d, raw_ref, bias_ref, rate_ref)
        mask = edge_mask(d, length, taps)
        before.append(doubled(jnp.where(mask, jnp.exp(-cumul) * step, 0.0)))
        after.append(doubled(jnp.exp(cumul)))
        write, read = projections(d, proj_ref)
        scores = dot(read, write, (((1,), (1,)), ((), ())))
        mixes.append(jnp.where(s <= t if d == 0 else s >= t, scores, 0.0).astype(BF16))
        skips.append(doubled(skip_ref[d : d + 1, :]))
        masks.append(mask)
    for j in range(width // chunk):
        lanes = slice(j * chunk, (j + 1) * chunk)
        x = x_ref[:, lanes].astype(F32)
        match = spread(2 * heads, heads, head, j * chunk, chunk)
        total = None
        for d in range(2):
            conved = conv_rows(d, x, cw_ref, cb_ref, lanes).astype(F32)
            scaled = (conved * dot(before[d], match)).astype(BF16)
            inner = dot(mixes[d], scaled) * dot(after[d], match)
            direct = jnp.where(masks[d], conved * dot(skips[d], match), 0.0)
            total = inner + direct if total is None else total + inner + direct
        y_ref[:, lanes] = total


def expand_rows(tiles, head, start, width):
    match = spread(LANES, LANES, head, start, width)
    wide = dot(jnp.concatenate(tiles, axis=0).astype(BF16), match)
    return [wide[i * SUB : (i + 1) * SUB] for i in range(len(tiles))]


def edge_state(d, window, wide, coef, heads, state, edge, cw_ref, cb_ref, lanes):
    conved = edge_conv(d, window, cw_ref, cb_ref, lanes).astype(F32)
    row = rows_of(window.shape)
    value = jnp.where(row < edge, conved * wide, 0.0).astype(BF16)
    write = coef[:, heads : heads + state]
    write = jnp.where(rows_of(write.shape) < edge, write, 0.0).astype(BF16)
    return dot(write, value, (((0,), (0,)), ((), ())))


def window_of(d, before, here, after, edge):
    row = rows_of(here.shape)
    up, down = SUB - edge, edge
    if d == 0:
        return jnp.where(row < edge, pltpu.roll(before, up, 0), pltpu.roll(here, down, 0))
    return jnp.where(row < edge, pltpu.roll(here, up, 0), pltpu.roll(after, down, 0))


def group_kernel(dims, cw_ref, cb_ref, *refs):
    group, count, head, heads, state, edge, axis = dims
    ins, refs = refs[:group], refs[group:]
    outs, refs = refs[: count - 1], refs[count - 1 :]
    own_ref, kept_ref, tiles_ref, wide_ref, slots = refs
    part = ins[0].shape[1]
    per_row = part // LANES
    place_in = lax.axis_index(axis)
    me, mine = lax.rem(place_in, group), lax.div(place_in, group)
    start = pl.multiple_of(me * part, LANES)
    lanes = pl.ds(start, part)
    for k in range(group):
        slots[partner(me, k, group)[0]] = ins[k][...]
    tiles = [slots[p, 2 * state :, :].astype(F32) for p in range(group)]
    row128 = rows_of((SUB, LANES))
    small, log_of = [], []
    for p in range(group):
        for d in range(2):
            base = d * edge
            rows = [fetch(tiles[p], base + j, per_row, 2 * edge) for j in range(edge)]
            at = 2 * edge + 3 * d
            log = sum(fetch(tiles[p], at + j, per_row, 2 * edge) for j in range(3))
            log_of.append(log)
            parts = [v.astype(F32) for v in split(jnp.exp(log), 2)]
            small.append(stacked(rows + parts))
    wide = expand_rows(small, head, start, part)
    zero = jnp.zeros((state, part), F32)
    totals, ends = [], []
    for d in range(2):
        order = range(group) if d == 0 else range(group - 1, -1, -1)
        running = zero
        for p in order:
            w = wide[2 * p + d]
            total = w[edge : edge + 1] + w[edge + 1 : edge + 2]
            kept = slots[p, d * state : (d + 1) * state, :].astype(F32)
            if p != order[0]:
                window = window_of(
                    d, tiles[p - 1] if d == 0 else None, tiles[p],
                    tiles[p + 1] if d == 1 else None, edge,
                )
                kept = kept + edge_state(
                    d, window, w, small[2 * p + d], heads, state, edge, cw_ref, cb_ref, lanes
                )
            kept_ref[d, p] = kept
            running = total * running + kept
            wide_ref[d, p] = w
        ends.append(running)
    for p in range(group):
        tiles_ref[p] = tiles[p]
    lane = lanes_of((SUB, LANES))
    row = rows_of((SUB, part))
    edges = jnp.where(row < edge, tiles[0], tiles[group - 1])
    messages = []
    for d in range(2):
        bound = 0 if d == 0 else group - 1
        others = [p for p in range(group) if p != bound]
        sum_log = log_of[2 * bound + d] * 0.0
        for p in others:
            sum_log = sum_log + log_of[2 * p + d]
        scale = jnp.where(lane < heads, jnp.exp(sum_log), 1.0)
        all_log = sum_log + log_of[2 * bound + d]
        sent = small[2 * bound + d] * scale
        logs = [v.astype(F32) for v in split(all_log, 3)]
        pieces, mine_pieces = [], []
        for i in range(per_row):
            cut = edges[:, i * LANES : (i + 1) * LANES]
            far = [sent[j : j + 1] for j in range(edge)] + logs
            near = [small[2 * bound + d][j : j + 1] for j in range(edge)] + logs
            clean = jnp.where(row128 < 2 * edge, cut, 0.0)
            pieces.append(place(clean, far, per_row, i, 2 * edge))
            mine_pieces.append(place(clean, near, per_row, i, 2 * edge))
        messages.append(jnp.concatenate(pieces, axis=1))
        own_ref[d] = jnp.concatenate(mine_pieces, axis=1)
    for k in range(1, count):
        forward = partner(mine, k, count)[1] > mine
        out_ref = outs[k - 1]
        out_ref[:state, :] = jnp.where(forward, ends[0], ends[1]).astype(BF16)
        out_ref[state:, :] = jnp.where(forward, messages[0], messages[1]).astype(BF16)


def enter_kernel(dims, cw_ref, cb_ref, *refs):
    group, count, head, heads, state, edge, axis = dims
    ins, refs = refs[: count - 1], refs[count - 1 :]
    (own_ref, kept_ref, tiles_ref, wide_ref), refs = refs[:4], refs[4:]
    outs, refs = refs[:group], refs[group:]
    far_ref, near_ref, slots = refs
    part = own_ref.shape[2]
    per_row = part // LANES
    place_in = lax.axis_index(axis)
    me, mine = lax.rem(place_in, group), lax.div(place_in, group)
    start = pl.multiple_of(me * part, LANES)
    lanes = pl.ds(start, part)
    for k in range(1, count):
        source = partner(mine, k, count)[0]
        far_ref[source] = ins[k - 1][:state, :].astype(F32)
        tile = ins[k - 1][state:, :].astype(F32)
        near_ref[0, source] = tile
        near_ref[1, source] = tile
    far_ref[mine] = jnp.zeros((state, part), F32)
    near_ref[0, mine] = own_ref[0]
    near_ref[1, mine] = own_ref[1]
    small = []
    for p in range(count):
        for d in range(2):
            tile = near_ref[d, p]
            rows = [fetch(tile, j, per_row, 2 * edge) for j in range(edge)]
            log = sum(fetch(tile, edge + j, per_row, 2 * edge) for j in range(3))
            parts = [v.astype(F32) for v in split(jnp.exp(log), 2)]
            small.append(stacked(rows + parts))
    wide = expand_rows(small, head, start, part)
    nothing = jnp.zeros((SUB, part), F32)
    row = rows_of((SUB, part))
    coming, bounds = [], []
    for d in range(2):
        order = range(count) if d == 0 else range(count - 1, -1, -1)
        running = jnp.zeros((state, part), F32)
        bound = jnp.zeros((state, part), F32)
        for p in order:
            w = wide[2 * p + d]
            before = near_ref[0, p - 1] if p > 0 else nothing
            after = near_ref[1, p + 1] if p < count - 1 else nothing
            window = window_of(d, before, near_ref[d, p], after, edge)
            added = edge_state(
                d, window, w, small[2 * p + d], heads, state, edge, cw_ref, cb_ref, lanes
            )
            total = w[edge : edge + 1] + w[edge + 1 : edge + 2]
            longer = total * running + (far_ref[p] + added)
            earlier = p < mine if d == 0 else p > mine
            running = jnp.where(earlier, longer, running)
            bound = jnp.where(mine == p, added, bound)
        coming.append(running)
        bounds.append(bound)
    for d in range(2):
        order = range(group) if d == 0 else range(group - 1, -1, -1)
        running = coming[d]
        for p in order:
            slots[p, d * state : (d + 1) * state, :] = running.astype(BF16)
            w = wide_ref[d, p]
            total = w[edge : edge + 1] + w[edge + 1 : edge + 2]
            kept = kept_ref[d, p]
            if p == order[0]:
                kept = kept + bounds[d]
            running = total * running + kept
    outer_before = jnp.where(mine > 0, near_ref[0, jnp.maximum(mine - 1, 0)], 0.0)
    outer_after = jnp.where(mine < count - 1, near_ref[1, jnp.minimum(mine + 1, count - 1)], 0.0)
    for p in range(group):
        before = tiles_ref[p - 1] if p > 0 else outer_before
        after = tiles_ref[p + 1] if p < group - 1 else outer_after
        halo = jnp.where(
            row < edge, pltpu.roll(before, SUB - edge, 0),
            jnp.where(row < 2 * edge, pltpu.roll(after, edge, 0), 0.0),
        )
        slots[p, 2 * state :, :] = halo.astype(BF16)
    for k in range(group):
        outs[k][...] = slots[partner(me, k, group)[1]]


def finish_kernel(
    dims, y_ref, gate_ref, x_ref, proj_ref, raw_ref, cw_ref, cb_ref, bias_ref, rate_ref,
    skip_ref, gain_ref, *refs
):
    group, head, chunk, axis = dims
    ins, (out_ref, held) = refs[:group], refs[group:]
    length, width = x_ref.shape
    heads = raw_ref.shape[1] // 2
    taps = cw_ref.shape[1]
    edge = taps - 1
    state = proj_ref.shape[1] // 4
    part = width // group
    me = lax.rem(lax.axis_index(axis), group)
    t, s = rows_of((length, SUB)), lanes_of((length, SUB))
    reads, after, before, skips = [], [], [], []
    for d in range(2):
        step, cumul = scan_parts(d, raw_ref, bias_ref, rate_ref)
        after.append(doubled(jnp.exp(cumul)))
        u = jnp.exp(-cumul) * step
        write, read = projections(d, proj_ref)
        write = write.astype(F32)
        if d == 0:
            u, write = u[:SUB], write[:SUB]
            allowed = (s <= t) & (s < edge)
        else:
            u = pltpu.roll(u[length - SUB :], edge, 0)
            write = pltpu.roll(write[length - SUB :], edge, 0)
            allowed = (s + length - edge >= t) & (s < edge)
        u = jnp.where(rows_of(u.shape) < edge, u, 0.0)
        before.append(doubled(u))
        scores = dot(read, write.astype(BF16), (((1,), (1,)), ((), ())))
        scores = jnp.where(allowed, scores, 0.0)
        reads.append(jnp.concatenate([read.astype(F32), scores], axis=1).astype(BF16))
        skips.append(doubled(skip_ref[d : d + 1, :]))
    squares = jnp.zeros((length, 1), F32)
    row = rows_of((SUB, chunk))
    for k in range(group):
        source = partner(me, k, group)[0]
        for j in range(part // chunk):
            start = pl.multiple_of(source * part + j * chunk, chunk)
            lanes = pl.ds(start, chunk)
            here = slice(j * chunk, (j + 1) * chunk)
            match = spread(2 * heads, heads, head, start, chunk)
            halo = ins[k][2 * state :, here].astype(F32)
            total = y_ref[:, lanes]
            for d in range(2):
                if d == 0:
                    near = x_ref[: 2 * SUB, lanes].astype(F32)[:SUB]
                    window = jnp.where(row < edge, halo, pltpu.roll(near, edge, 0))
                else:
                    near = x_ref[length - 2 * SUB :, lanes].astype(F32)[SUB:]
                    window = jnp.where(row < edge, pltpu.roll(near, edge, 0), halo)
                conved = edge_conv(d, window, cw_ref, cb_ref, lanes).astype(F32)
                conved = jnp.where(row < edge, conved, 0.0)
                scaled = conved * dot(before[d], match)
                coming = ins[k][d * state : (d + 1) * state, here].astype(F32)
                right = jnp.concatenate([coming, scaled], axis=0).astype(BF16)
                added = dot(reads[d], right) * dot(after[d], match)
                direct = conved * dot(skips[d], match)
                if d == 0:
                    direct = jnp.concatenate(
                        [direct, jnp.zeros((length - SUB, chunk), F32)], axis=0
                    )
                else:
                    direct = jnp.concatenate(
                        [jnp.zeros((length - SUB, chunk), F32), pltpu.roll(direct, SUB - edge, 0)],
                        axis=0,
                    )
                total = total + added + direct
            gated = total * silu(gate_ref[:, lanes].astype(F32))
            held[:, lanes] = gated
            squares = squares + jnp.sum(gated * gated, axis=1, keepdims=True)
    scale = lax.rsqrt(squares / width + 1e-05)
    for j in range(width // chunk):
        lanes = slice(j * chunk, (j + 1) * chunk)
        out_ref[:, lanes] = (held[:, lanes] * scale * gain_ref[:, lanes]).astype(BF16)


def call(body, outs, args, scratch=(), flops=0, name=None):
    vmem = pl.BlockSpec(memory_space=pltpu.VMEM)
    return pl.pallas_call(
        body,
        out_shape=outs,
        in_specs=[vmem] * len(args),
        out_specs=jax.tree.map(lambda _: vmem, outs),
        scratch_shapes=list(scratch),
        cost_estimate=pl.CostEstimate(flops=flops, bytes_accessed=1 << 20, transcendentals=0),
        name=name,
    )(*args)


def local(
    axis, ranks, inner_acts, gate_acts, state_proj, step_raw, conv_weight, conv_bias, step_bias,
    decay_rate, skip_gain, norm_gain,
):
    length, width = inner_acts.shape
    heads = step_raw.shape[1] // 2
    head = width // heads
    state = state_proj.shape[1] // 4
    edge = conv_weight.shape[1] - 1
    group = 1
    for g in range(1, ranks + 1):
        fits = width % (g * LANES) == 0 and (
            2 * edge + coef_rows(2 * edge + 6, width // (g * LANES)) <= SUB
        )
        if ranks % g == 0 and g * g <= ranks and fits:
            group = g
    count = ranks // group
    part = width // group
    chunk = 2 * LANES if part % (2 * LANES) == 0 else LANES
    tile_rows = SUB
    shape = jax.ShapeDtypeStruct
    dims = (group, head, chunk, axis)
    params = (conv_weight, conv_bias, step_bias, decay_rate)
    tokens = (inner_acts, state_proj, step_raw)
    big = length * width
    message = shape((2 * state + tile_rows, part), BF16)
    ends = call(
        functools.partial(ends_kernel, dims), [message] * group, tokens + params,
        flops=big * 400, name="ends",
    )
    got = [ends[0]] + [
        lax.ppermute(ends[k], axis, pairs(k, group, 1, ranks)) for k in range(1, group)
    ]
    inside = call(
        functools.partial(inside_kernel, dims), shape((length, width), F32),
        tokens + params + (skip_gain,), flops=big * 800, name="inside",
    )
    wide_dims = (group, count, head, heads, state, edge, axis)
    outs = call(
        functools.partial(group_kernel, wide_dims),
        [shape((state + tile_rows, part), BF16)] * (count - 1)
        + [
            shape((2, tile_rows, part), F32),
            shape((2, group, state, part), F32),
            shape((group, tile_rows, part), F32),
            shape((2, group, tile_rows, part), F32),
        ],
        (conv_weight, conv_bias, *got),
        scratch=[pltpu.VMEM((group, 2 * state + tile_rows, part), BF16)],
        flops=big * 100, name="group",
    )
    sent, rest = outs[: count - 1], outs[count - 1 :]
    far = [
        lax.ppermute(sent[k - 1], axis, pairs(k, count, group, ranks)) for k in range(1, count)
    ]
    enter = call(
        functools.partial(enter_kernel, wide_dims), [message] * group,
        (conv_weight, conv_bias, *far, *rest),
        scratch=[
            pltpu.VMEM((count, state, part), F32),
            pltpu.VMEM((2, count, tile_rows, part), F32),
            pltpu.VMEM((group, 2 * state + tile_rows, part), BF16),
        ],
        flops=big * 100, name="enter",
    )
    back = [enter[0]] + [
        lax.ppermute(enter[k], axis, pairs(k, group, 1, ranks)) for k in range(1, group)
    ]
    return call(
        functools.partial(finish_kernel, dims), shape((length, width), BF16),
        (inside, gate_acts, *tokens, *params, skip_gain, norm_gain[None, :], *back),
        scratch=[pltpu.VMEM((length, width), F32)], flops=big * 800, name="finish",
    )


def solution(mesh):
    axis = "seq"
    rows = P(("img", axis), None)
    return jax.shard_map(
        functools.partial(local, axis, mesh.shape[axis]),
        mesh=mesh,
        in_specs=(rows,) * 4 + (P(),) * 6,
        out_specs=rows,
        check_vma=False,
    )
```

time: 296 us -> 53.4 us (0.18); the launches traced: 293 us -> 53 us
  local copies, waits for them, and re-layouts: 83.6 us -> 4.77 us
  blocking collectives: 78.1 us -> 0 us
  other arithmetic: 45 us -> 0 us
  waiting for transfers between devices: 49 us -> 11.1 us
  Pallas kernels: 0 us -> 24.8 us
  matrix products: 15.6 us -> 0 us
  between operations: 13.9 us -> 0.05 us
  starting transfers between devices: 6.86 us -> 12.4 us
    all_gather x2 -> x0, blocking collectives: 78.1 us -> none  [prefix(): pieces = jax.tree.map(lambda part: lax.all_gather(part, axis), value)]
    all_gather x2 -> x0, waiting for transfers between devices: 48.9 us -> none  [prefix(): pieces = jax.tree.map(lambda part: lax.all_gather(part, axis), value)]
    slice x12 -> x0, local copies, waits for them, and re-layouts: 39.6 us -> none  [the longest x5 36.6 us: convolve(): window[start:start + length].astype(jnp.float32)]
    select_n x30 -> x0, other arithmetic: 34.6 us -> none  [lap(): jnp.where(position < mine, new, old)]
    pallas_call x0 -> x5, Pallas kernels: none -> 24.8 us  [call(): pl.pallas_call(body, out_shape=outs, in_specs=[vmem] * len(args), out_spe...]
    mul x33 -> x0, local copies, waits for them, and re-layouts: 21.8 us -> none  [the longest x30 20.5 us: combine_carry(): later[0][:, None, None] * earlier[1] + later[1]]
    dot_general x8 -> x0, matrix products: 15.6 us -> none  [the longest x2 7.22 us: inter_terms(): jnp.einsum('tn,hpn->thp', read_rows.astype(jnp.float32), incoming, precis...]
    rev x3 -> x0, local copies, waits for them, and re-layouts: 14.4 us -> none  [the longest x1 7.85 us: local(): (backward_base + inter_terms(backward_log, flipped_proj[:, 3 * state_dim:...]
  transfers between devices with their start and end apart: 4 -> 9, of which waited for: 2 -> 5; matrix products, arithmetic and copies ran while one was open for 25% -> 0% of each run, Pallas kernels for 0% -> 15%
where the time goes in v1:
time: 53.4 us; the launch traced here: 53 us
  Pallas kernels  24.8 us (46%)
  starting transfers between devices  12.4 us (23%)
  waiting for transfers between devices  11.1 us (21%)
  local copies, waits for them, and re-layouts  4.77 us (9%)
    pallas_call x5, Pallas kernels, call(): pl.pallas_call(body, out_shape=outs, in_specs=[vmem] * len(args), out_spe...  24.8 us
    ppermute x3, waiting for transfers between devices, local(): lax.ppermute(sent[k - 1], axis, pairs(k, count, group, ranks))  5.74 us
    ppermute x3, waiting for transfers between devices, local(): lax.ppermute(ends[k], axis, pairs(k, group, 1, ranks))  5.32 us
    unnamed x20, local copies, waits for them, and re-layouts  4.77 us
    ppermute x3, starting transfers between devices, local(): lax.ppermute(ends[k], axis, pairs(k, group, 1, ranks))  4.49 us
    ppermute x3, starting transfers between devices, local(): lax.ppermute(sent[k - 1], axis, pairs(k, count, group, ranks))  4.39 us
    ppermute x3, starting transfers between devices, local(): lax.ppermute(enter[k], axis, pairs(k, group, 1, ranks))  3.49 us
  transfers between devices with their start and end apart: 9, of which 5 were waited for; matrix products, arithmetic and copies ran while one was open for 0% of the time, Pallas kernels for 15%

profile of v1, /device:TPU:0, one launch (start us, length us, event | category | flops | bytes accessed | tf_op | source)
XLA Modules:
  0.0 53.0 jit_solution(6689668067682995764)
XLA Ops:
  0.0 1.4 %copy.11.proj_ref = bf16[128,64]{1,0:T(8,128)(2,1)} copy(bf16[128,64]{0,1:T(8,128)(2,1)} %param.12) | data formatting | bytes 32768 | tf_op args[2]
  1.4 1.5 %copy.12.raw_ref = bf16[128,96]{1,0:T(8,128)(2,1)} copy(bf16[128,96]{0,1:T(8,128)(2,1)} %param.13) | data formatting | bytes 49152 | tf_op args[3]
  2.9 6.2 %ends.1 = (bf16[40,768]{1,0:T(8,128)(2,1)}, bf16[40,768]{1,0:T(8,128)(2,1)}, bf16[40,768]{1,0:T(8,128)(2,1)}, bf16[40,768]{1,0:T(8,128)(2,1)}) custom-call(bf16[128,3072]{1,0:T(8,128)(2,1)} %x_ref.5, bf16[128,64]{1,0:T(8,128)(2,1)} %copy.11.proj_ref, bf16[128,96]{1,0:T(8,128)(2,1)} %copy.12.raw_ref, f32[2,4,3072]{2,1,0:T(4,128)} %cw_ref.9, ...), custom_call_target="tpu_custom_call" | custom-call | flops 157286400 | bytes 1048576 | tf_op jit(solution)/shard_map/ends/pallas_call | solution.py:493
  9.1 3.0 %collective-permute-start = (bf16[40,768]{1,0:T(8,128)(2,1)}, bf16[40,768]{1,0:T(8,128)(2,1)S(1)}, u32[]{:S(2)}, u32[]{:S(2)}) collective-permute-start(bf16[40,768]{1,0:T(8,128)(2,1)} %get-tuple-element.21), channel_id=1, source_target_pairs={{0,2},{2,0},{4,6},{6,4},{8,10},{10,8},{12,14},{14,12},{16,18},{18,... | collective-permute-start | bytes 184328 | tf_op jit(solution)/shard_map/ppermute | solution.py:535
  12.1 1.5 %collective-permute-start.1 = (bf16[40,768]{1,0:T(8,128)(2,1)}, bf16[40,768]{1,0:T(8,128)(2,1)S(1)}, u32[]{:S(2)}, u32[]{:S(2)}) collective-permute-start(bf16[40,768]{1,0:T(8,128)(2,1)} %get-tuple-element.22), channel_id=1, source_target_pairs={{0,4},{2,6},{4,0},{6,2},{8,12},{10,14},{12,8},{14,10},{16,20},{18,... | collective-permute-start | bytes 184328 | tf_op jit(solution)/shard_map/ppermute | solution.py:535
  13.6 0.0 collective-permute-start.2
  13.6 1.1 %collective-permute-done.refs_1_ = bf16[40,768]{1,0:T(8,128)(2,1)S(1)} collective-permute-done((bf16[40,768]{1,0:T(8,128)(2,1)}, bf16[40,768]{1,0:T(8,128)(2,1)S(1)}, u32[]{:S(2)}, u32[]{:S(2)}) %collective-permute-start) | collective-permute-done | bytes 61472 | tf_op jit(solution)/shard_map/ppermute | solution.py:535
  14.7 1.8 %collective-permute-done.1.refs_2_ = bf16[40,768]{1,0:T(8,128)(2,1)S(1)} collective-permute-done((bf16[40,768]{1,0:T(8,128)(2,1)}, bf16[40,768]{1,0:T(8,128)(2,1)S(1)}, u32[]{:S(2)}, u32[]{:S(2)}) %collective-permute-start.1) | collective-permute-done | bytes 61472 | tf_op jit(solution)/shard_map/ppermute | solution.py:535
  16.5 2.4 %collective-permute-done.2.refs_3_ = bf16[40,768]{1,0:T(8,128)(2,1)S(1)} collective-permute-done((bf16[40,768]{1,0:T(8,128)(2,1)}, bf16[40,768]{1,0:T(8,128)(2,1)S(1)}, u32[]{:S(2)}, u32[]{:S(2)}) %collective-permute-start.2) | collective-permute-done | bytes 61472 | tf_op jit(solution)/shard_map/ppermute | solution.py:535
  18.9 0.0 copy-done
  18.9 0.6 %copy-done.2 = bf16[40,768]{1,0:T(8,128)(2,1)} copy-done((bf16[40,768]{1,0:T(8,128)(2,1)}, bf16[40,768]{1,0:T(8,128)(2,1)S(1)}, u32[]{:S(2)}) %copy-start.2) | copy-done | bytes 61464
  19.6 2.2 %group.1 = (bf16[24,768]{1,0:T(8,128)(2,1)}, bf16[24,768]{1,0:T(8,128)(2,1)}, bf16[24,768]{1,0:T(8,128)(2,1)}, f32[2,8,768]{2,1,0:T(8,128)}, f32[2,4,16,768]{3,2...) custom-call(f32[2,4,3072]{2,1,0:T(4,128)} %cw_ref.9, f32[2,3072]{1,0:T(2,128)} %cb_ref.9, ...), custom_call_target="tpu_custom_call" | custom-call | flops 39321600 | bytes 1048576 | tf_op jit(solution)/shard_map/group/pallas_call | solution.py:493
  21.7 1.6 %collective-permute-start.3 = (bf16[24,768]{1,0:T(8,128)(2,1)}, bf16[24,768]{1,0:T(8,128)(2,1)S(1)}, u32[]{:S(2)}, u32[]{:S(2)}) collective-permute-start(bf16[24,768]{1,0:T(8,128)(2,1)} %get-tuple-element.24), channel_id=1, source_target_pairs={{0,8},{2,10},{4,12},{6,14},{8,0},{10,2},{12,4},{14,6},{16,24},{18,... | collective-permute-start | bytes 110600 | tf_op jit(solution)/shard_map/ppermute | solution.py:557
  23.3 2.6 %collective-permute-start.4 = (bf16[24,768]{1,0:T(8,128)(2,1)}, bf16[24,768]{1,0:T(8,128)(2,1)S(1)}, u32[]{:S(2)}, u32[]{:S(2)}) collective-permute-start(bf16[24,768]{1,0:T(8,128)(2,1)} %get-tuple-element.25), channel_id=1, source_target_pairs={{0,16},{2,18},{4,20},{6,22},{8,24},{10,26},{12,28},{14,30},{16,0},... | collective-permute-start | bytes 110600 | tf_op jit(solution)/shard_map/ppermute | solution.py:557
  25.9 0.2 collective-permute-start.5
  26.1 0.0 collective-permute-done.3.refs_0_
  26.1 3.0 %collective-permute-done.4.refs_1_ = bf16[24,768]{1,0:T(8,128)(2,1)S(1)} collective-permute-done((bf16[24,768]{1,0:T(8,128)(2,1)}, bf16[24,768]{1,0:T(8,128)(2,1)S(1)}, u32[]{:S(2)}, u32[]{:S(2)}) %collective-permute-start.4) | collective-permute-done | bytes 36896 | tf_op jit(solution)/shard_map/ppermute | solution.py:557
  29.1 2.8 %collective-permute-done.5.refs_2_ = bf16[24,768]{1,0:T(8,128)(2,1)S(1)} collective-permute-done((bf16[24,768]{1,0:T(8,128)(2,1)}, bf16[24,768]{1,0:T(8,128)(2,1)S(1)}, u32[]{:S(2)}, u32[]{:S(2)}) %collective-permute-start.5) | collective-permute-done | bytes 36896 | tf_op jit(solution)/shard_map/ppermute | solution.py:557
  31.9 0.0 copy-done.6
  31.9 0.6 %copy-done.8 = bf16[24,768]{1,0:T(8,128)(2,1)} copy-done((bf16[24,768]{1,0:T(8,128)(2,1)}, bf16[24,768]{1,0:T(8,128)(2,1)S(1)}, u32[]{:S(2)}) %copy-start.8) | copy-done | bytes 36888
  32.5 2.4 %enter.1 = (bf16[40,768]{1,0:T(8,128)(2,1)}, bf16[40,768]{1,0:T(8,128)(2,1)}, bf16[40,768]{1,0:T(8,128)(2,1)}, bf16[40,768]{1,0:T(8,128)(2,1)}) custom-call(f32[2,4,3072]{2,1,0:T(4,128)} %cw_ref.9, f32[2,3072]{1,0:T(2,128)} %cb_ref.9, bf16[24,768]{1,0:T(8,128)(2,1)} %copy-done.6, bf16[24,768]{1,0:T(8,128)(2,1)} %copy-done.7, bf16[24,768]{1,0:T(8,128)(2,1)} %copy-done.8, ...), custom_call_target="tpu_custom_call" | custom-call | flops 39321600 | bytes 1048576 | tf_op jit(solution)/shard_map/enter/pallas_call | solution.py:493
  34.9 0.5 %collective-permute-start.6 = (bf16[40,768]{1,0:T(8,128)(2,1)}, bf16[40,768]{1,0:T(8,128)(2,1)S(1)}, u32[]{:S(2)}, u32[]{:S(2)}) collective-permute-start(bf16[40,768]{1,0:T(8,128)(2,1)} %get-tuple-element.32), channel_id=1, source_target_pairs={{0,2},{2,0},{4,6},{6,4},{8,10},{10,8},{12,14},{14,12},{16,18},{18,... | collective-permute-start | bytes 184328 | tf_op jit(solution)/shard_map/ppermute | solution.py:570
  35.4 0.5 collective-permute-start.7
  36.0 2.4 %collective-permute-start.8 = (bf16[40,768]{1,0:T(8,128)(2,1)}, bf16[40,768]{1,0:T(8,128)(2,1)S(1)}, u32[]{:S(2)}, u32[]{:S(2)}) collective-permute-start(bf16[40,768]{1,0:T(8,128)(2,1)} %get-tuple-element.34), channel_id=1, source_target_pairs={{0,6},{2,4},{4,2},{6,0},{8,14},{10,12},{12,10},{14,8},{16,22},{18,... | collective-permute-start | bytes 184328 | tf_op jit(solution)/shard_map/ppermute | solution.py:570
  38.4 8.2 %inside.1.y_ref = f32[128,3072]{1,0:T(8,128)} custom-call(bf16[128,3072]{1,0:T(8,128)(2,1)} %x_ref.5, bf16[128,64]{1,0:T(8,128)(2,1)} %copy.11.proj_ref, bf16[128,96]{1,0:T(8,128)(2,1)} %copy.12.raw_ref, f32[2,4,3072]{2,1,0:T(4,128)} %cw_ref.9, f32[2,3072]{1,0:T(2,128)} %cb_ref.9, f32[2,48]{1,0:T(2,128)} %bias_ref.5, f32[2,48]{1,0:T(2,128)} %rate_ref.5, ...), custom_call_target="tpu_custom_call" | custom-call | flops 314572800 | bytes 1048576 | tf_op jit(solution)/shard_map/inside/pallas_call | solution.py:493
  46.6 0.0 collective-permute-done.6.refs_1_
  46.6 0.0 collective-permute-done.7.refs_2_
  46.6 0.0 copy-start.4
  46.6 0.0 collective-permute-done.8.refs_3_
  46.6 0.6 %copy-done.3 = bf16[40,768]{1,0:T(8,128)(2,1)} copy-done((bf16[40,768]{1,0:T(8,128)(2,1)}, bf16[40,768]{1,0:T(8,128)(2,1)S(1)}, u32[]{:S(2)}) %copy-start.3) | copy-done | bytes 61464
  47.2 0.0 copy-done.4
  47.3 5.8 %finish.1 = bf16[128,3072]{1,0:T(8,128)(2,1)} custom-call(f32[128,3072]{1,0:T(8,128)} %inside.1.y_ref, bf16[128,3072]{1,0:T(8,128)(2,1)} %gate_ref.1, bf16[128,3072]{1,0:T(8,128)(2,1)} %x_ref.5, bf16[128,64]{1,0:T(8,128)(2,1)} %copy.11.proj_ref, bf16[128,96]{1,0:T(8,128)(2,1)} %copy.12.raw_ref, f32[2,4,3072]{2,1,0:T(4,128)} %cw_ref.9, f32[2,3072]{1,0:T(2,128)} %cb_ref.9, ...), custom_call_target="tpu_custom_call" | custom-call | flops 314572800 | bytes 1048576 | tf_op jit(solution)/shard_map/finish/pallas_call | solution.py:493
  (11 shorter events, 0.0 us)
Async XLA Ops:
  9.1 5.6 %collective-permute-start = (bf16[40,768]{1,0:T(8,128)(2,1)}, bf16[40,768]{1,0:T(8,128)(2,1)S(1)}, u32[]{:S(2)}, u32[]{:S(2)}) collective-permute-start(bf16[40,768]{1,0:T(8,128)(2,1)} %get-tuple-element.21), channel_id=1, source_target_pairs={{0,2},{2,0},{4,6},{6,4},{8,10},{10,8},{12,14},{14,12},{16,18},{18,... | collective-permute-start | bytes 184328 | tf_op jit(solution)/shard_map/ppermute | solution.py:535
  12.1 4.4 %collective-permute-start.1 = (bf16[40,768]{1,0:T(8,128)(2,1)}, bf16[40,768]{1,0:T(8,128)(2,1)S(1)}, u32[]{:S(2)}, u32[]{:S(2)}) collective-permute-start(bf16[40,768]{1,0:T(8,128)(2,1)} %get-tuple-element.22), channel_id=1, source_target_pairs={{0,4},{2,6},{4,0},{6,2},{8,12},{10,14},{12,8},{14,10},{16,20},{18,... | collective-permute-start | bytes 184328 | tf_op jit(solution)/shard_map/ppermute | solution.py:535
  13.6 5.3 %collective-permute-start.2 = (bf16[40,768]{1,0:T(8,128)(2,1)}, bf16[40,768]{1,0:T(8,128)(2,1)S(1)}, u32[]{:S(2)}, u32[]{:S(2)}) collective-permute-start(bf16[40,768]{1,0:T(8,128)(2,1)} %get-tuple-element.23), channel_id=1, source_target_pairs={{0,6},{2,4},{4,2},{6,0},{8,14},{10,12},{12,10},{14,8},{16,22},{18,... | collective-permute-start | bytes 184328 | tf_op jit(solution)/shard_map/ppermute | solution.py:535
  14.7 4.2 %copy-start = (bf16[40,768]{1,0:T(8,128)(2,1)}, bf16[40,768]{1,0:T(8,128)(2,1)S(1)}, u32[]{:S(2)}) copy-start(bf16[40,768]{1,0:T(8,128)(2,1)S(1)} %collective-permute-done.refs_1_) | copy-start | bytes 184324
  16.5 2.4 %copy-start.1 = (bf16[40,768]{1,0:T(8,128)(2,1)}, bf16[40,768]{1,0:T(8,128)(2,1)S(1)}, u32[]{:S(2)}) copy-start(bf16[40,768]{1,0:T(8,128)(2,1)S(1)} %collective-permute-done.1.refs_2_) | copy-start | bytes 184324
  18.9 0.6 %copy-start.2 = (bf16[40,768]{1,0:T(8,128)(2,1)}, bf16[40,768]{1,0:T(8,128)(2,1)S(1)}, u32[]{:S(2)}) copy-start(bf16[40,768]{1,0:T(8,128)(2,1)S(1)} %collective-permute-done.2.refs_3_) | copy-start | bytes 184324
  21.7 4.4 %collective-permute-start.3 = (bf16[24,768]{1,0:T(8,128)(2,1)}, bf16[24,768]{1,0:T(8,128)(2,1)S(1)}, u32[]{:S(2)}, u32[]{:S(2)}) collective-permute-start(bf16[24,768]{1,0:T(8,128)(2,1)} %get-tuple-element.24), channel_id=1, source_target_pairs={{0,8},{2,10},{4,12},{6,14},{8,0},{10,2},{12,4},{14,6},{16,24},{18,... | collective-permute-start | bytes 110600 | tf_op jit(solution)/shard_map/ppermute | solution.py:557
  23.3 5.8 %collective-permute-start.4 = (bf16[24,768]{1,0:T(8,128)(2,1)}, bf16[24,768]{1,0:T(8,128)(2,1)S(1)}, u32[]{:S(2)}, u32[]{:S(2)}) collective-permute-start(bf16[24,768]{1,0:T(8,128)(2,1)} %get-tuple-element.25), channel_id=1, source_target_pairs={{0,16},{2,18},{4,20},{6,22},{8,24},{10,26},{12,28},{14,30},{16,0},... | collective-permute-start | bytes 110600 | tf_op jit(solution)/shard_map/ppermute | solution.py:557
  25.9 6.0 %collective-permute-start.5 = (bf16[24,768]{1,0:T(8,128)(2,1)}, bf16[24,768]{1,0:T(8,128)(2,1)S(1)}, u32[]{:S(2)}, u32[]{:S(2)}) collective-permute-start(bf16[24,768]{1,0:T(8,128)(2,1)} %get-tuple-element.26), channel_id=1, source_target_pairs={{0,24},{2,26},{4,28},{6,30},{8,16},{10,18},{12,20},{14,22},{16,8},... | collective-permute-start | bytes 110600 | tf_op jit(solution)/shard_map/ppermute | solution.py:557
  26.1 5.7 %copy-start.6 = (bf16[24,768]{1,0:T(8,128)(2,1)}, bf16[24,768]{1,0:T(8,128)(2,1)S(1)}, u32[]{:S(2)}) copy-start(bf16[24,768]{1,0:T(8,128)(2,1)S(1)} %collective-permute-done.3.refs_0_) | copy-start | bytes 110596
  29.1 2.8 %copy-start.7 = (bf16[24,768]{1,0:T(8,128)(2,1)}, bf16[24,768]{1,0:T(8,128)(2,1)S(1)}, u32[]{:S(2)}) copy-start(bf16[24,768]{1,0:T(8,128)(2,1)S(1)} %collective-permute-done.4.refs_1_) | copy-start | bytes 110596
  31.9 0.6 %copy-start.8 = (bf16[24,768]{1,0:T(8,128)(2,1)}, bf16[24,768]{1,0:T(8,128)(2,1)S(1)}, u32[]{:S(2)}) copy-start(bf16[24,768]{1,0:T(8,128)(2,1)S(1)} %collective-permute-done.5.refs_2_) | copy-start | bytes 110596
  34.9 11.7 %collective-permute-start.6 = (bf16[40,768]{1,0:T(8,128)(2,1)}, bf16[40,768]{1,0:T(8,128)(2,1)S(1)}, u32[]{:S(2)}, u32[]{:S(2)}) collective-permute-start(bf16[40,768]{1,0:T(8,128)(2,1)} %get-tuple-element.32), channel_id=1, source_target_pairs={{0,2},{2,0},{4,6},{6,4},{8,10},{10,8},{12,14},{14,12},{16,18},{18,... | collective-permute-start | bytes 184328 | tf_op jit(solution)/shard_map/ppermute | solution.py:570
  35.4 11.2 %collective-permute-start.7 = (bf16[40,768]{1,0:T(8,128)(2,1)}, bf16[40,768]{1,0:T(8,128)(2,1)S(1)}, u32[]{:S(2)}, u32[]{:S(2)}) collective-permute-start(bf16[40,768]{1,0:T(8,128)(2,1)} %get-tuple-element.33), channel_id=1, source_target_pairs={{0,4},{2,6},{4,0},{6,2},{8,12},{10,14},{12,8},{14,10},{16,20},{18,... | collective-permute-start | bytes 184328 | tf_op jit(solution)/shard_map/ppermute | solution.py:570
  36.0 10.7 %collective-permute-start.8 = (bf16[40,768]{1,0:T(8,128)(2,1)}, bf16[40,768]{1,0:T(8,128)(2,1)S(1)}, u32[]{:S(2)}, u32[]{:S(2)}) collective-permute-start(bf16[40,768]{1,0:T(8,128)(2,1)} %get-tuple-element.34), channel_id=1, source_target_pairs={{0,6},{2,4},{4,2},{6,0},{8,14},{10,12},{12,10},{14,8},{16,22},{18,... | collective-permute-start | bytes 184328 | tf_op jit(solution)/shard_map/ppermute | solution.py:570
  46.6 0.6 %copy-start.3 = (bf16[40,768]{1,0:T(8,128)(2,1)}, bf16[40,768]{1,0:T(8,128)(2,1)S(1)}, u32[]{:S(2)}) copy-start(bf16[40,768]{1,0:T(8,128)(2,1)S(1)} %collective-permute-done.6.refs_1_) | copy-start | bytes 184324
  46.6 0.7 %copy-start.4 = (bf16[40,768]{1,0:T(8,128)(2,1)}, bf16[40,768]{1,0:T(8,128)(2,1)S(1)}, u32[]{:S(2)}) copy-start(bf16[40,768]{1,0:T(8,128)(2,1)S(1)} %collective-permute-done.7.refs_2_) | copy-start | bytes 184324
  46.6 0.6 %copy-start.5 = (bf16[40,768]{1,0:T(8,128)(2,1)}, bf16[40,768]{1,0:T(8,128)(2,1)S(1)}, u32[]{:S(2)}) copy-start(bf16[40,768]{1,0:T(8,128)(2,1)S(1)} %collective-permute-done.8.refs_3_) | copy-start | bytes 184324
